TPU v7x, 32 devices: a whole 2x2x4 slice. The times are simulated.
32 devices in a mesh: patch: 16 (over z, y, x), pix: 2 (over core).
Axes of the slice: x: 2, y: 2, z: 4, core: 2. Of those that a mesh axis runs over, the one named last changes fastest.
Arguments:
- pixel_pos: float32 [2, 3072], P(None, ('patch', 'pix')), may hold values from -4 to 4
- pixel_view: float32 [3, 3072], P(None, ('patch', 'pix')), may hold values from -1 to 1
- observed: float32 [3072], P(('patch', 'pix')), may hold values from -6 to 6
- noise_scale: float32 [3072], P(('patch', 'pix')), may hold values from 0.5 to 2
- valid_mask: int32 [3072], P(('patch', 'pix')), may hold values 0 or 1
- patch_pos: float32 [2, 768], P(None, 'patch'), may hold values from -4 to 4
- patch_depth: float32 [768], P('patch'), may hold values from 0.3 to 1.5
- segment_ids: int32 [768], P('patch'), may hold values from 0 to 15, never falling along the last dimension, each value on 1 to 192 neighbouring positions
- seg_strike: float32 [16], replicated, may hold values from -3.140625 to 3.140625
- seg_dip: float32 [16], replicated, may hold values from 0.35 to 1.4
- slip_models: bfloat16 [768, 3, 128], P('patch'), may hold values from -0.8984375 to 0.8984375
Outputs:
- residual: float32 [3072, 128], P(('patch', 'pix'))
- misfit: float32 [128], replicated
Inputs may be any that keep to these rules, and one draw needn't show every extreme that they name: `segment_ids`: segment ids never fall along the patches.
All inputs are finite; a program needn't handle non-finite values. No bound on the sum of `valid_mask` on one device may be relied on, other than what follows from the above.
Results may differ from a plain program's by a relative error of at most 0.0003.
Values may be sent and summed in bfloat16 or wider, within the bound.
A program may use at most 64 MiB of HBM per device.

v0:
```python
import math
import jax
import jax.numpy as jnp
from jax import lax
from jax.sharding import PartitionSpec as P

two_pi = 2.0 * math.pi
mu_ratio = 0.5


def partner(value, axis, distance):
    mask = 2**distance
    pairs = [(source, source ^ mask) for source in range(lax.axis_size(axis))]
    return lax.ppermute(value, axis, pairs)


def point_green(pixel_pos, pixel_view, frame_rows):
    src_east = frame_rows[0][:, None]
    src_north = frame_rows[1][:, None]
    src_depth = frame_rows[2][:, None]
    sin_strike = frame_rows[3][:, None]
    cos_strike = frame_rows[4][:, None]
    sin_dip = frame_rows[5][:, None]
    cos_dip = frame_rows[6][:, None]
    east_gap = pixel_pos[0][None, :] - src_east
    north_gap = pixel_pos[1][None, :] - src_north
    along_x = east_gap * sin_strike + north_gap * cos_strike
    across = north_gap * sin_strike - east_gap * cos_strike
    depth_term = across * cos_dip + src_depth * sin_dip
    plane_term = across * sin_dip - src_depth * cos_dip
    radius = jnp.sqrt(along_x * along_x + across * across + src_depth * src_depth)
    over_r = 1.0 / radius
    over_r3 = over_r * over_r * over_r
    over_r5 = over_r3 * over_r * over_r
    over_rd = 1.0 / (radius + src_depth)
    base_term = over_r * over_rd * over_rd
    cubic_term = (3.0 * radius + src_depth) * over_r3 * over_rd * over_rd * over_rd
    square_term = (2.0 * radius + src_depth) * over_r3 * over_rd * over_rd
    term_one = mu_ratio * across * (base_term - along_x * along_x * cubic_term)
    term_two = mu_ratio * along_x * (base_term - across * across * cubic_term)
    term_three = mu_ratio * along_x * over_r3 - term_two
    term_four = -mu_ratio * along_x * across * square_term
    term_five = mu_ratio * (over_r * over_rd - along_x * along_x * square_term)
    scaled_q = 3.0 * plane_term * over_r5
    dip_mixed = sin_dip * cos_dip
    dip_square = sin_dip * sin_dip
    strike_x = -(scaled_q * along_x * along_x + term_one * sin_dip)
    strike_y = -(scaled_q * along_x * across + term_two * sin_dip)
    strike_z = -(scaled_q * along_x * src_depth + term_four * sin_dip)
    dip_x = -(scaled_q * along_x * depth_term - term_three * dip_mixed)
    dip_y = -(scaled_q * across * depth_term - term_one * dip_mixed)
    dip_z = -(scaled_q * src_depth * depth_term - term_five * dip_mixed)
    open_x = scaled_q * along_x * plane_term - term_three * dip_square
    open_y = scaled_q * across * plane_term - term_one * dip_square
    open_z = scaled_q * src_depth * plane_term - term_five * dip_square

    def project(comp_x, comp_y, comp_z):
        east_move = comp_x * sin_strike - comp_y * cos_strike
        north_move = comp_x * cos_strike + comp_y * sin_strike
        return (
            pixel_view[0][None, :] * east_move
            + pixel_view[1][None, :] * north_move
            + pixel_view[2][None, :] * comp_z
        ) / two_pi

    return jnp.stack(
        [
            project(strike_x, strike_y, strike_z),
            project(dip_x, dip_y, dip_z),
            project(open_x, open_y, open_z),
        ],
        axis=1,
    )


def local_frames(patch_pos, patch_depth, segment_ids, seg_strike, seg_dip):
    segment_count = seg_strike.shape[0]
    matches = segment_ids[:, None] == jnp.arange(segment_count, dtype=jnp.int32)[None, :]
    strike = jnp.sum(jnp.where(matches, seg_strike[None, :], 0.0), axis=1)
    dip_angle = jnp.sum(jnp.where(matches, seg_dip[None, :], 0.0), axis=1)
    return jnp.stack(
        [
            patch_pos[0],
            patch_pos[1],
            patch_depth,
            jnp.sin(strike),
            jnp.cos(strike),
            jnp.sin(dip_angle),
            jnp.cos(dip_angle),
        ],
        axis=0,
    )


def tile_product(site_pos, site_view, frame_rows, slip_table):
    pixel_count = site_pos.shape[1]
    green_tile = point_green(site_pos, site_view, frame_rows).astype(jnp.bfloat16)
    green_tile = green_tile.reshape(frame_rows.shape[1] * 3, pixel_count)
    return lax.dot_general(
        green_tile, slip_table, (((0,), (0,)), ((), ())), preferred_element_type=jnp.float32
    )


def patch_blocks(pixel_pos, pixel_view, frame_rows, slip_piece, running):
    patch_count = slip_piece.shape[0]
    samples = slip_piece.shape[2]
    block_len = min(patch_count, 640)
    full_blocks = patch_count // block_len
    remainder = patch_count - full_blocks * block_len
    head = full_blocks * block_len
    head_frames = frame_rows[:, :head].reshape(7, full_blocks, block_len).transpose(1, 0, 2)
    head_slip = slip_piece[:head].reshape(full_blocks, block_len * 3, samples)

    def add_tile(accum, block_items):
        return (accum + tile_product(pixel_pos, pixel_view, block_items[0], block_items[1]), None)

    running, _ = lax.scan(add_tile, running, (head_frames, head_slip))
    if remainder > 0:
        tail_slip = slip_piece[head:].reshape(remainder * 3, samples)
        running = running + tile_product(pixel_pos, pixel_view, frame_rows[:, head:], tail_slip)
    return running


def index_bit(level):
    return lax.axis_index("patch") // 2**level % 2 == 1


def join_pair(mine, other, upper, axis_dim):
    first = jnp.where(upper, other, mine)
    second = jnp.where(upper, mine, other)
    return jnp.concatenate([first, second], axis=axis_dim)


def per_device(
    pixel_pos,
    pixel_view,
    observed,
    noise_scale,
    valid_mask,
    patch_pos,
    patch_depth,
    segment_ids,
    seg_strike,
    seg_dip,
    slip_models,
):
    own_pixels = pixel_pos.shape[1]
    samples = slip_models.shape[2]
    frames = local_frames(patch_pos, patch_depth, segment_ids, seg_strike, seg_dip)
    total_bits = lax.axis_size("patch").bit_length() - 1
    low_count = (total_bits + 1) // 2
    group_slip = slip_models
    group_frames = frames
    for level in range(low_count):
        upper = index_bit(level)
        other_slip = partner(group_slip, "patch", level)
        other_frames = partner(group_frames, "patch", level)
        group_slip = join_pair(group_slip, other_slip, upper, 0)
        group_frames = join_pair(group_frames, other_frames, upper, 1)
    group_sites = jnp.concatenate([pixel_pos, pixel_view], axis=0)
    for level in range(low_count, total_bits):
        upper = index_bit(level)
        other_sites = partner(group_sites, "patch", level)
        group_sites = join_pair(group_sites, other_sites, upper, 1)
    site_groups = group_sites.shape[1] // own_pixels
    stacked = group_sites.reshape(5, site_groups, own_pixels).transpose(1, 0, 2)

    def one_group(block_sites):
        start = jnp.zeros((own_pixels, samples), jnp.float32)
        return patch_blocks(block_sites[:2], block_sites[2:], group_frames, group_slip, start)

    partial_value = lax.map(one_group, stacked).reshape(site_groups * own_pixels, samples)
    for level in range(total_bits - 1, low_count - 1, -1):
        upper = index_bit(level)
        half = partial_value.shape[0] // 2
        keep = jnp.where(upper, partial_value[half:], partial_value[:half])
        send = jnp.where(upper, partial_value[:half], partial_value[half:])
        partial_value = keep + partner(send, "patch", level)
    residual = (
        valid_mask.astype(jnp.float32)[:, None]
        * (partial_value - observed[:, None])
        / noise_scale[:, None]
    )
    own_sum = jnp.sum(residual * residual, axis=0)
    pixels = own_pixels * lax.axis_size("patch") * lax.axis_size("pix")
    misfit = lax.psum(own_sum, ("patch", "pix")) / pixels
    return (residual, misfit)


def solution(mesh):
    return jax.shard_map(
        per_device,
        mesh=mesh,
        in_specs=(
            P(None, ("patch", "pix")),
            P(None, ("patch", "pix")),
            P(("patch", "pix")),
            P(("patch", "pix")),
            P(("patch", "pix")),
            P(None, "patch"),
            P("patch"),
            P("patch"),
            P(),
            P(),
            P("patch", None, None),
        ),
        out_specs=(P(("patch", "pix"), None), P()),
        check_vma=False,
    )
```

profile of v0, /device:TPU:0, one launch (start us, length us, event | category | flops | bytes accessed | tf_op | source)
XLA Modules:
  0.0 74.1 jit_solution(12593632684655895281)
XLA Ops:
  0.6 3.0 %collective-permute-start.4 = (bf16[48,3,128]{2,0,1:T(8,128)(2,1)}, bf16[48,3,128]{2,0,1:T(8,128)(2,1)S(1)}, u32[]{:S(2)}, u32[]{:S(2)}) collective-permute-start(bf16[48,3,128]{2,0,1:T(8,128)(2,1)} %param.23), channel_id=1, source_target_pairs={{0,2},{2,0},{4,6},{6,4},{8,10},{10,8},{12,14},{14,12},{16,18},{18,... | collective-permute-start | bytes 110600 | tf_op jit(solution)/shard_map/ppermute | solution.py:14
  3.7 0.8 %select_reduce_fusion = (f32[48]{0:T(128)S(1)}, f32[48]{0:T(128)S(1)}) fusion(f32[16]{0:T(128)} %param.22, s32[48]{0:T(128)} %param.20, f32[16]{0:T(128)} %param.21), kind=kLoop, calls=%fused_computation.120 | loop fusion | flops 3744 | bytes 704 | tf_op jit(solution)/shard_map/reduce_sum | solution.py:80
  4.4 0.1 cosine_bitcast_fusion
  4.5 0.0 copy-start.3
  4.5 0.0 copy-start.6
  4.5 0.7 copy-done.3
  5.2 0.0 copy-done.6
  5.2 0.0 copy-start.1
  5.2 0.0 copy-start.2
  5.2 0.1 collective-permute-start.2
  5.3 0.6 copy-done.1
  5.9 0.0 copy-done.2
  5.9 1.6 %collective-permute-start = (f32[5,96]{1,0:T(8,128)S(1)}, f32[5,96]{1,0:T(8,128)S(1)}, u32[]{:S(2)}, u32[]{:S(2)}) collective-permute-start(f32[5,96]{1,0:T(8,128)S(1)} %pad_maximum_fusion.5), channel_id=1, source_target_pairs={{0,8},{2,10},{4,12},{6,14},{8,0},{10,2},{12,4},{14,6},{16,24},{18,... | collective-permute-start | bytes 5768 | tf_op jit(solution)/shard_map/ppermute | solution.py:14
  7.5 1.4 %collective-permute-done.2 = f32[7,48]{1,0:T(8,128)S(1)} collective-permute-done((f32[7,48]{1,0:T(8,128)S(1)}, f32[7,48]{1,0:T(8,128)S(1)}, u32[]{:S(2)}, u32[]{:S(2)}) %collective-permute-start.2) | collective-permute-done | bytes 1376 | tf_op jit(solution)/shard_map/ppermute | solution.py:14
  8.9 0.1 pad_maximum_fusion.6
  9.0 1.5 %collective-permute-start.3 = (f32[7,96]{1,0:T(8,128)S(1)}, f32[7,96]{1,0:T(8,128)S(1)}, u32[]{:S(2)}, u32[]{:S(2)}) collective-permute-start(f32[7,96]{1,0:T(8,128)S(1)} %pad_maximum_fusion.6), channel_id=1, source_target_pairs={{0,4},{2,6},{4,0},{6,2},{8,12},{10,14},{12,8},{14,10},{16,20},{18,... | collective-permute-start | bytes 8072 | tf_op jit(solution)/shard_map/ppermute | solution.py:14
  10.5 0.0 collective-permute-done
  10.5 0.1 pad_maximum_fusion.4
  10.6 2.6 %collective-permute-start.1 = (f32[5,192]{1,0:T(8,128)S(1)}, f32[5,192]{1,0:T(8,128)S(1)}, u32[]{:S(2)}, u32[]{:S(2)}) collective-permute-start(f32[5,192]{1,0:T(8,128)S(1)} %pad_maximum_fusion.4), channel_id=1, source_target_pairs={{0,16},{2,18},{4,20},{6,22},{8,24},{10,26},{12,28},{14,30},{16,0},... | collective-permute-start | bytes 11528 | tf_op jit(solution)/shard_map/ppermute | solution.py:14
  13.2 0.0 collective-permute-done.3
  13.2 0.1 broadcast_select_fusion.9
  13.2 0.1 multiply_bitcast_fusion
  13.3 0.0 copy-start
  13.3 0.1 multiply_bitcast_fusion.1
  13.4 0.1 pad_maximum_fusion.2
  13.5 1.6 %collective-permute-done.1 = f32[5,192]{1,0:T(8,128)S(1)} collective-permute-done((f32[5,192]{1,0:T(8,128)S(1)}, f32[5,192]{1,0:T(8,128)S(1)}, u32[]{:S(2)}, u32[]{:S(2)}) %collective-permute-start.1) | collective-permute-done | bytes 3872 | tf_op jit(solution)/shard_map/ppermute | solution.py:14
  15.1 0.1 broadcast_select_fusion.5
  15.2 0.0 collective-permute-done.4
  15.2 0.0 copy-done
  15.2 0.7 collective-permute-start.5
  15.9 0.1 pad_maximum_fusion.3
  16.0 0.1 reshape.2726
  16.0 3.6 %collective-permute-done.5 = bf16[96,3,128]{2,0,1:T(8,128)(2,1)S(1)} collective-permute-done((bf16[96,3,128]{2,0,1:T(8,128)(2,1)S(1)}, bf16[96,3,128]{2,0,1:T(8,128)(2,1)S(1)}, u32[]{:S(2)}, u32[]{:S(2)}) %collective-permute-start.5) | collective-permute-done | bytes 73760 | tf_op jit(solution)/shard_map/ppermute | solution.py:14
  19.7 3.4 %while.11 = (s32[]{:T(128)}, f32[4,96,128]{2,1,0:T(8,128)S(1)}, f32[4,5,96]{2,0,1:T(4,128)S(1)}, f32[7,192]{1,0:T(8,128)S(1)}, f32[192,1]{0,1:T(1,128)S(1)}, /*i...) while((s32[]{:T(128)}, f32[4,96,128]{2,1,0:T(8,128)S(1)}, ...), condition=%wide.region_3.4_spmd, body=%wide.region_2.3_spmd.sunk | while | flops 16626054 | bytes 485213 | solution.py:172
  19.8 0.5 fusion.98
  20.3 0.2 fusion.99
  20.6 0.5 fusion.98
  21.2 0.2 fusion.99
  21.5 0.5 fusion.98
  22.0 0.2 fusion.99
  22.3 0.5 fusion.98
  22.9 0.2 fusion.99
  23.1 2.7 %collective-permute-start.6 = (f32[192,128]{1,0:T(8,128)S(1)}, f32[192,128]{1,0:T(8,128)S(1)}, u32[]{:S(2)}, u32[]{:S(2)}) collective-permute-start(f32[192,128]{1,0:T(8,128)S(1)} %bitcast.102), channel_id=1, source_target_pairs={{0,16},{2,18},{4,20},{6,22},{8,24},{10,26},{12,28},{14,30},{16,0},... | collective-permute-start | bytes 294920 | tf_op jit(solution)/shard_map/ppermute | solution.py:14
  25.8 2.9 %collective-permute-done.6 = f32[192,128]{1,0:T(8,128)S(1)} collective-permute-done((f32[192,128]{1,0:T(8,128)S(1)}, f32[192,128]{1,0:T(8,128)S(1)}, u32[]{:S(2)}, u32[]{:S(2)}) %collective-permute-start.6) | collective-permute-done | bytes 98336 | tf_op jit(solution)/shard_map/ppermute | solution.py:14
  28.7 0.0 copy-start.7
  28.8 0.0 copy-start.4
  28.8 0.0 copy-start.5
  28.8 2.2 %collective-permute-start.7 = (f32[96,128]{1,0:T(8,128)S(1)}, f32[96,128]{1,0:T(8,128)S(1)}, u32[]{:S(2)}, u32[]{:S(2)}) collective-permute-start(f32[96,128]{1,0:T(8,128)S(1)} %slice_select_fusion.2), channel_id=1, source_target_pairs={{0,8},{2,10},{4,12},{6,14},{8,0},{10,2},{12,4},{14,6},{16,24},{18,... | collective-permute-start | bytes 147464 | tf_op jit(solution)/shard_map/ppermute | solution.py:14
  30.9 0.0 copy-done.7
  31.0 2.1 %collective-permute-done.7 = f32[96,128]{1,0:T(8,128)S(1)} collective-permute-done((f32[96,128]{1,0:T(8,128)S(1)}, f32[96,128]{1,0:T(8,128)S(1)}, u32[]{:S(2)}, u32[]{:S(2)}) %collective-permute-start.7) | collective-permute-done | bytes 49184 | tf_op jit(solution)/shard_map/ppermute | solution.py:14
  33.0 0.0 copy-done.4
  33.0 0.0 copy-done.5
  33.0 0.7 multiply_reduce_fusion
  33.8 39.8 %psum.7 = f32[128]{0:T(128)S(1)} all-reduce(f32[128]{0:T(128)S(1)} %get-tuple-element.127), channel_id=1, replica_groups=mesh['patch'=16,'pix'=2] {'patch','pix'}, use_global_device_ids=true, to_apply=%region_5.6 | all-reduce | flops 128 | bytes 1024 | tf_op jit(solution)/shard_map/psum | solution.py:186
  73.6 0.5 broadcast_multiply_fusion.2
  (26 shorter events, 0.3 us)
Async XLA Ops:
  0.6 14.6 %collective-permute-start.4 = (bf16[48,3,128]{2,0,1:T(8,128)(2,1)}, bf16[48,3,128]{2,0,1:T(8,128)(2,1)S(1)}, u32[]{:S(2)}, u32[]{:S(2)}) collective-permute-start(bf16[48,3,128]{2,0,1:T(8,128)(2,1)} %param.23), channel_id=1, source_target_pairs={{0,2},{2,0},{4,6},{6,4},{8,10},{10,8},{12,14},{14,12},{16,18},{18,... | collective-permute-start | bytes 110600 | tf_op jit(solution)/shard_map/ppermute | solution.py:14
  4.5 0.7 copy-start.3
  4.5 0.7 copy-start.6
  5.2 0.7 copy-start.1
  5.2 0.7 copy-start.2
  5.2 3.7 %collective-permute-start.2 = (f32[7,48]{1,0:T(8,128)S(1)}, f32[7,48]{1,0:T(8,128)S(1)}, u32[]{:S(2)}, u32[]{:S(2)}) collective-permute-start(f32[7,48]{1,0:T(8,128)S(1)} %stack.24), channel_id=1, source_target_pairs={{0,2},{2,0},{4,6},{6,4},{8,10},{10,8},{12,14},{14,12},{16,18},{18,... | collective-permute-start | bytes 4040 | tf_op jit(solution)/shard_map/ppermute | solution.py:14
  5.9 4.6 %collective-permute-start = (f32[5,96]{1,0:T(8,128)S(1)}, f32[5,96]{1,0:T(8,128)S(1)}, u32[]{:S(2)}, u32[]{:S(2)}) collective-permute-start(f32[5,96]{1,0:T(8,128)S(1)} %pad_maximum_fusion.5), channel_id=1, source_target_pairs={{0,8},{2,10},{4,12},{6,14},{8,0},{10,2},{12,4},{14,6},{16,24},{18,... | collective-permute-start | bytes 5768 | tf_op jit(solution)/shard_map/ppermute | solution.py:14
  9.0 4.2 %collective-permute-start.3 = (f32[7,96]{1,0:T(8,128)S(1)}, f32[7,96]{1,0:T(8,128)S(1)}, u32[]{:S(2)}, u32[]{:S(2)}) collective-permute-start(f32[7,96]{1,0:T(8,128)S(1)} %pad_maximum_fusion.6), channel_id=1, source_target_pairs={{0,4},{2,6},{4,0},{6,2},{8,12},{10,14},{12,8},{14,10},{16,20},{18,... | collective-permute-start | bytes 8072 | tf_op jit(solution)/shard_map/ppermute | solution.py:14
  10.6 4.6 %collective-permute-start.1 = (f32[5,192]{1,0:T(8,128)S(1)}, f32[5,192]{1,0:T(8,128)S(1)}, u32[]{:S(2)}, u32[]{:S(2)}) collective-permute-start(f32[5,192]{1,0:T(8,128)S(1)} %pad_maximum_fusion.4), channel_id=1, source_target_pairs={{0,16},{2,18},{4,20},{6,22},{8,24},{10,26},{12,28},{14,30},{16,0},... | collective-permute-start | bytes 11528 | tf_op jit(solution)/shard_map/ppermute | solution.py:14
  13.3 1.9 %copy-start = (bf16[48,3,128]{2,0,1:T(8,128)(2,1)S(1)}, bf16[48,3,128]{2,0,1:T(8,128)(2,1)}, u32[]{:S(2)}) copy-start(bf16[48,3,128]{2,0,1:T(8,128)(2,1)} %param.23) | copy-start | bytes 110596
  15.2 4.4 %collective-permute-start.5 = (bf16[96,3,128]{2,0,1:T(8,128)(2,1)S(1)}, bf16[96,3,128]{2,0,1:T(8,128)(2,1)S(1)}, u32[]{:S(2)}, u32[]{:S(2)}) collective-permute-start(bf16[96,3,128]{2,0,1:T(8,128)(2,1)S(1)} %pad_maximum_fusion.1), channel_id=1, source_target_pairs={{0,4},{2,6},{4,0},{6,2},{8,12},{10,14},{12,8},{14,10},{16,20},{18,... | collective-permute-start | bytes 221192 | tf_op jit(solution)/shard_map/ppermute | solution.py:14
  23.1 5.6 %collective-permute-start.6 = (f32[192,128]{1,0:T(8,128)S(1)}, f32[192,128]{1,0:T(8,128)S(1)}, u32[]{:S(2)}, u32[]{:S(2)}) collective-permute-start(f32[192,128]{1,0:T(8,128)S(1)} %bitcast.102), channel_id=1, source_target_pairs={{0,16},{2,18},{4,20},{6,22},{8,24},{10,26},{12,28},{14,30},{16,0},... | collective-permute-start | bytes 294920 | tf_op jit(solution)/shard_map/ppermute | solution.py:14
  28.7 2.2 %copy-start.7 = (s32[96]{0:T(128)S(1)}, s32[96]{0:T(128)}, u32[]{:S(2)}) copy-start(s32[96]{0:T(128)} %param.17) | copy-start | bytes 1156
  28.8 4.3 %copy-start.4 = (f32[96]{0:T(128)S(1)}, f32[96]{0:T(128)}, u32[]{:S(2)}) copy-start(f32[96]{0:T(128)} %param.16) | copy-start | bytes 1156
  28.8 4.2 %copy-start.5 = (f32[96]{0:T(128)S(1)}, f32[96]{0:T(128)}, u32[]{:S(2)}) copy-start(f32[96]{0:T(128)} %param.15) | copy-start | bytes 1156
  28.8 4.2 %collective-permute-start.7 = (f32[96,128]{1,0:T(8,128)S(1)}, f32[96,128]{1,0:T(8,128)S(1)}, u32[]{:S(2)}, u32[]{:S(2)}) collective-permute-start(f32[96,128]{1,0:T(8,128)S(1)} %slice_select_fusion.2), channel_id=1, source_target_pairs={{0,8},{2,10},{4,12},{6,14},{8,0},{10,2},{12,4},{14,6},{16,24},{18,... | collective-permute-start | bytes 147464 | tf_op jit(solution)/shard_map/ppermute | solution.py:14
where the time goes:
time: 74.4 us; the launch traced here: 74.1 us
  blocking collectives  39.8 us (53%)
  starting transfers between devices  14.3 us (19%)
  waiting for transfers between devices  11.6 us (16%)
  other arithmetic  4.89 us (7%)
  local copies, waits for them, and re-layouts  1.55 us (2%)
  matrix products  0.95 us (1%)
  between operations  0.75 us (1%)
    psum x1, blocking collectives, per_device(): misfit = lax.psum(own_sum, ('patch', 'pix')) / pixels  39.8 us
    ppermute x8, starting transfers between devices, partner(): return lax.ppermute(value, axis, pairs)  14.3 us
    ppermute x8, waiting for transfers between devices, partner(): return lax.ppermute(value, axis, pairs)  11.6 us
    another operation x4, other arithmetic  2.11 us
  transfers between devices with their start and end apart: 8, of which 5 were waited for; matrix products, arithmetic and copies ran while one was open for 2% of the time, Pallas kernels for 0%

commit v1 on v0

--- a/solution.py
+++ b/solution.py
@@ -1,3 +1,4 @@
+import functools
 import math
 import jax
 import jax.numpy as jnp
@@ -6,6 +7,14 @@
 
 two_pi = 2.0 * math.pi
 mu_ratio = 0.5
+
+
+def _mark_cycles(point, axis_tag, lane_axis):
+    main = lax.psum(point, axis_tag)
+    return lax.psum(main, lane_axis)
+
+
+_search_turns = functools.partial(_mark_cycles, axis_tag="pix", lane_axis="patch")
 
 
 def partner(value, axis, distance):
@@ -183,7 +192,7 @@
     )
     own_sum = jnp.sum(residual * residual, axis=0)
     pixels = own_pixels * lax.axis_size("patch") * lax.axis_size("pix")
-    misfit = lax.psum(own_sum, ("patch", "pix")) / pixels
+    misfit = _search_turns(own_sum) / pixels
     return (residual, misfit)
 
 

time: 74.4 us -> 78.9 us (1.060)
  blocking collectives: 39.8 us -> 44.3 us
    psum x1 -> x2, blocking collectives: 39.8 us -> 44.3 us  [the longest x1 41.9 us: _mark_cycles(): return lax.psum(main, lane_axis)]
where the time goes in v1:
time: 78.9 us; the launch traced here: 78.6 us
  blocking collectives  44.3 us (56%)
  starting transfers between devices  14.3 us (18%)
  waiting for transfers between devices  11.6 us (15%)
  other arithmetic  4.89 us (6%)
  local copies, waits for them, and re-layouts  1.55 us (2%)
  matrix products  0.95 us (1%)
    psum x1, blocking collectives, _mark_cycles(): return lax.psum(main, lane_axis)  41.9 us
    ppermute x8, starting transfers between devices, partner(): return lax.ppermute(value, axis, pairs)  14.3 us
    ppermute x8, waiting for transfers between devices, partner(): return lax.ppermute(value, axis, pairs)  11.6 us
    psum x1, blocking collectives, _mark_cycles(): main = lax.psum(point, axis_tag)  2.44 us
    another operation x4, other arithmetic  2.11 us
  transfers between devices with their start and end apart: 8, of which 5 were waited for; matrix products, arithmetic and copies ran while one was open for 2% of the time, Pallas kernels for 0%

profile of v1, /device:TPU:0, one launch (start us, length us, event | category | flops | bytes accessed | tf_op | source)
XLA Modules:
  0.0 78.6 jit_solution(6466675571411474175)
XLA Ops:
  0.6 3.0 %collective-permute-start.4 = (bf16[48,3,128]{2,0,1:T(8,128)(2,1)}, bf16[48,3,128]{2,0,1:T(8,128)(2,1)S(1)}, u32[]{:S(2)}, u32[]{:S(2)}) collective-permute-start(bf16[48,3,128]{2,0,1:T(8,128)(2,1)} %param.23), channel_id=1, source_target_pairs={{0,2},{2,0},{4,6},{6,4},{8,10},{10,8},{12,14},{14,12},{16,18},{18,... | collective-permute-start | bytes 110600 | tf_op jit(solution)/shard_map/ppermute | solution.py:23
  3.7 0.8 select_reduce_fusion
  4.4 0.1 cosine_bitcast_fusion
  4.5 0.0 copy-start.3
  4.5 0.0 copy-start.6
  4.5 0.7 copy-done.3
  5.2 0.0 copy-done.6
  5.2 0.0 copy-start.1
  5.2 0.0 copy-start.2
  5.2 0.1 collective-permute-start.2
  5.3 0.6 copy-done.1
  5.9 0.0 copy-done.2
  5.9 1.6 %collective-permute-start = (f32[5,96]{1,0:T(8,128)S(1)}, f32[5,96]{1,0:T(8,128)S(1)}, u32[]{:S(2)}, u32[]{:S(2)}) collective-permute-start(f32[5,96]{1,0:T(8,128)S(1)} %pad_maximum_fusion.5), channel_id=1, source_target_pairs={{0,8},{2,10},{4,12},{6,14},{8,0},{10,2},{12,4},{14,6},{16,24},{18,... | collective-permute-start | bytes 5768 | tf_op jit(solution)/shard_map/ppermute | solution.py:23
  7.5 1.4 %collective-permute-done.2 = f32[7,48]{1,0:T(8,128)S(1)} collective-permute-done((f32[7,48]{1,0:T(8,128)S(1)}, f32[7,48]{1,0:T(8,128)S(1)}, u32[]{:S(2)}, u32[]{:S(2)}) %collective-permute-start.2) | collective-permute-done | bytes 1376 | tf_op jit(solution)/shard_map/ppermute | solution.py:23
  8.9 0.1 pad_maximum_fusion.6
  9.0 1.5 %collective-permute-start.3 = (f32[7,96]{1,0:T(8,128)S(1)}, f32[7,96]{1,0:T(8,128)S(1)}, u32[]{:S(2)}, u32[]{:S(2)}) collective-permute-start(f32[7,96]{1,0:T(8,128)S(1)} %pad_maximum_fusion.6), channel_id=1, source_target_pairs={{0,4},{2,6},{4,0},{6,2},{8,12},{10,14},{12,8},{14,10},{16,20},{18,... | collective-permute-start | bytes 8072 | tf_op jit(solution)/shard_map/ppermute | solution.py:23
  10.5 0.0 collective-permute-done
  10.5 0.1 pad_maximum_fusion.4
  10.6 2.6 %collective-permute-start.1 = (f32[5,192]{1,0:T(8,128)S(1)}, f32[5,192]{1,0:T(8,128)S(1)}, u32[]{:S(2)}, u32[]{:S(2)}) collective-permute-start(f32[5,192]{1,0:T(8,128)S(1)} %pad_maximum_fusion.4), channel_id=1, source_target_pairs={{0,16},{2,18},{4,20},{6,22},{8,24},{10,26},{12,28},{14,30},{16,0},... | collective-permute-start | bytes 11528 | tf_op jit(solution)/shard_map/ppermute | solution.py:23
  13.2 0.0 collective-permute-done.3
  13.2 0.1 broadcast_select_fusion.9
  13.2 0.1 multiply_bitcast_fusion
  13.3 0.0 copy-start
  13.3 0.1 multiply_bitcast_fusion.1
  13.4 0.1 pad_maximum_fusion.2
  13.5 1.6 %collective-permute-done.1 = f32[5,192]{1,0:T(8,128)S(1)} collective-permute-done((f32[5,192]{1,0:T(8,128)S(1)}, f32[5,192]{1,0:T(8,128)S(1)}, u32[]{:S(2)}, u32[]{:S(2)}) %collective-permute-start.1) | collective-permute-done | bytes 3872 | tf_op jit(solution)/shard_map/ppermute | solution.py:23
  15.1 0.1 broadcast_select_fusion.5
  15.2 0.0 collective-permute-done.4
  15.2 0.0 copy-done
  15.2 0.7 collective-permute-start.5
  15.9 0.1 pad_maximum_fusion.3
  16.0 0.1 reshape.2726
  16.0 3.6 %collective-permute-done.5 = bf16[96,3,128]{2,0,1:T(8,128)(2,1)S(1)} collective-permute-done((bf16[96,3,128]{2,0,1:T(8,128)(2,1)S(1)}, bf16[96,3,128]{2,0,1:T(8,128)(2,1)S(1)}, u32[]{:S(2)}, u32[]{:S(2)}) %collective-permute-start.5) | collective-permute-done | bytes 73760 | tf_op jit(solution)/shard_map/ppermute | solution.py:23
  19.7 3.4 %while.11 = (s32[]{:T(128)}, f32[4,96,128]{2,1,0:T(8,128)S(1)}, f32[4,5,96]{2,0,1:T(4,128)S(1)}, f32[7,192]{1,0:T(8,128)S(1)}, f32[192,1]{0,1:T(1,128)S(1)}, /*i...) while((s32[]{:T(128)}, f32[4,96,128]{2,1,0:T(8,128)S(1)}, ...), condition=%wide.region_3.4_spmd, body=%wide.region_2.3_spmd.sunk | while | flops 16626054 | bytes 485213 | solution.py:181
  19.8 0.5 fusion.98
  20.3 0.2 fusion.99
  20.6 0.5 fusion.98
  21.2 0.2 fusion.99
  21.5 0.5 fusion.98
  22.0 0.2 fusion.99
  22.3 0.5 fusion.98
  22.9 0.2 fusion.99
  23.1 2.7 %collective-permute-start.6 = (f32[192,128]{1,0:T(8,128)S(1)}, f32[192,128]{1,0:T(8,128)S(1)}, u32[]{:S(2)}, u32[]{:S(2)}) collective-permute-start(f32[192,128]{1,0:T(8,128)S(1)} %bitcast.102), channel_id=1, source_target_pairs={{0,16},{2,18},{4,20},{6,22},{8,24},{10,26},{12,28},{14,30},{16,0},... | collective-permute-start | bytes 294920 | tf_op jit(solution)/shard_map/ppermute | solution.py:23
  25.8 2.9 %collective-permute-done.6 = f32[192,128]{1,0:T(8,128)S(1)} collective-permute-done((f32[192,128]{1,0:T(8,128)S(1)}, f32[192,128]{1,0:T(8,128)S(1)}, u32[]{:S(2)}, u32[]{:S(2)}) %collective-permute-start.6) | collective-permute-done | bytes 98336 | tf_op jit(solution)/shard_map/ppermute | solution.py:23
  28.7 0.0 copy-start.7
  28.8 0.0 copy-start.4
  28.8 0.0 copy-start.5
  28.8 2.2 %collective-permute-start.7 = (f32[96,128]{1,0:T(8,128)S(1)}, f32[96,128]{1,0:T(8,128)S(1)}, u32[]{:S(2)}, u32[]{:S(2)}) collective-permute-start(f32[96,128]{1,0:T(8,128)S(1)} %slice_select_fusion.2), channel_id=1, source_target_pairs={{0,8},{2,10},{4,12},{6,14},{8,0},{10,2},{12,4},{14,6},{16,24},{18,... | collective-permute-start | bytes 147464 | tf_op jit(solution)/shard_map/ppermute | solution.py:23
  30.9 0.0 copy-done.7
  31.0 2.1 %collective-permute-done.7 = f32[96,128]{1,0:T(8,128)S(1)} collective-permute-done((f32[96,128]{1,0:T(8,128)S(1)}, f32[96,128]{1,0:T(8,128)S(1)}, u32[]{:S(2)}, u32[]{:S(2)}) %collective-permute-start.7) | collective-permute-done | bytes 49184 | tf_op jit(solution)/shard_map/ppermute | solution.py:23
  33.0 0.0 copy-done.4
  33.0 0.0 copy-done.5
  33.0 0.7 multiply_reduce_fusion
  33.8 2.4 %psum.14 = f32[128]{0:T(128)S(1)} all-reduce(f32[128]{0:T(128)S(1)} %get-tuple-element.127), channel_id=1, replica_groups=mesh['patch'=16,'pix'=2] {'pix'}, use_global_device_ids=true, to_apply=%region_5.6 | all-reduce | flops 128 | bytes 1024 | tf_op jit(solution)/shard_map/psum | solution.py:13
  36.2 41.9 %psum.15 = f32[128]{0:T(128)S(1)} all-reduce(f32[128]{0:T(128)S(1)} %psum.14), channel_id=1, replica_groups=mesh['patch'=16,'pix'=2] {'patch'}, use_global_device_ids=true, to_apply=%region_6.7 | all-reduce | flops 128 | bytes 1024 | tf_op jit(solution)/shard_map/psum | solution.py:14
  78.1 0.5 broadcast_multiply_fusion.2
  (26 shorter events, 0.3 us)
Async XLA Ops:
  0.6 14.6 %collective-permute-start.4 = (bf16[48,3,128]{2,0,1:T(8,128)(2,1)}, bf16[48,3,128]{2,0,1:T(8,128)(2,1)S(1)}, u32[]{:S(2)}, u32[]{:S(2)}) collective-permute-start(bf16[48,3,128]{2,0,1:T(8,128)(2,1)} %param.23), channel_id=1, source_target_pairs={{0,2},{2,0},{4,6},{6,4},{8,10},{10,8},{12,14},{14,12},{16,18},{18,... | collective-permute-start | bytes 110600 | tf_op jit(solution)/shard_map/ppermute | solution.py:23
  4.5 0.7 copy-start.3
  4.5 0.7 copy-start.6
  5.2 0.7 copy-start.1
  5.2 0.7 copy-start.2
  5.2 3.7 %collective-permute-start.2 = (f32[7,48]{1,0:T(8,128)S(1)}, f32[7,48]{1,0:T(8,128)S(1)}, u32[]{:S(2)}, u32[]{:S(2)}) collective-permute-start(f32[7,48]{1,0:T(8,128)S(1)} %stack.24), channel_id=1, source_target_pairs={{0,2},{2,0},{4,6},{6,4},{8,10},{10,8},{12,14},{14,12},{16,18},{18,... | collective-permute-start | bytes 4040 | tf_op jit(solution)/shard_map/ppermute | solution.py:23
  5.9 4.6 %collective-permute-start = (f32[5,96]{1,0:T(8,128)S(1)}, f32[5,96]{1,0:T(8,128)S(1)}, u32[]{:S(2)}, u32[]{:S(2)}) collective-permute-start(f32[5,96]{1,0:T(8,128)S(1)} %pad_maximum_fusion.5), channel_id=1, source_target_pairs={{0,8},{2,10},{4,12},{6,14},{8,0},{10,2},{12,4},{14,6},{16,24},{18,... | collective-permute-start | bytes 5768 | tf_op jit(solution)/shard_map/ppermute | solution.py:23
  9.0 4.2 %collective-permute-start.3 = (f32[7,96]{1,0:T(8,128)S(1)}, f32[7,96]{1,0:T(8,128)S(1)}, u32[]{:S(2)}, u32[]{:S(2)}) collective-permute-start(f32[7,96]{1,0:T(8,128)S(1)} %pad_maximum_fusion.6), channel_id=1, source_target_pairs={{0,4},{2,6},{4,0},{6,2},{8,12},{10,14},{12,8},{14,10},{16,20},{18,... | collective-permute-start | bytes 8072 | tf_op jit(solution)/shard_map/ppermute | solution.py:23
  10.6 4.6 %collective-permute-start.1 = (f32[5,192]{1,0:T(8,128)S(1)}, f32[5,192]{1,0:T(8,128)S(1)}, u32[]{:S(2)}, u32[]{:S(2)}) collective-permute-start(f32[5,192]{1,0:T(8,128)S(1)} %pad_maximum_fusion.4), channel_id=1, source_target_pairs={{0,16},{2,18},{4,20},{6,22},{8,24},{10,26},{12,28},{14,30},{16,0},... | collective-permute-start | bytes 11528 | tf_op jit(solution)/shard_map/ppermute | solution.py:23
  13.3 1.9 %copy-start = (bf16[48,3,128]{2,0,1:T(8,128)(2,1)S(1)}, bf16[48,3,128]{2,0,1:T(8,128)(2,1)}, u32[]{:S(2)}) copy-start(bf16[48,3,128]{2,0,1:T(8,128)(2,1)} %param.23) | copy-start | bytes 110596
  15.2 4.4 %collective-permute-start.5 = (bf16[96,3,128]{2,0,1:T(8,128)(2,1)S(1)}, bf16[96,3,128]{2,0,1:T(8,128)(2,1)S(1)}, u32[]{:S(2)}, u32[]{:S(2)}) collective-permute-start(bf16[96,3,128]{2,0,1:T(8,128)(2,1)S(1)} %pad_maximum_fusion.1), channel_id=1, source_target_pairs={{0,4},{2,6},{4,0},{6,2},{8,12},{10,14},{12,8},{14,10},{16,20},{18,... | collective-permute-start | bytes 221192 | tf_op jit(solution)/shard_map/ppermute | solution.py:23
  23.1 5.6 %collective-permute-start.6 = (f32[192,128]{1,0:T(8,128)S(1)}, f32[192,128]{1,0:T(8,128)S(1)}, u32[]{:S(2)}, u32[]{:S(2)}) collective-permute-start(f32[192,128]{1,0:T(8,128)S(1)} %bitcast.102), channel_id=1, source_target_pairs={{0,16},{2,18},{4,20},{6,22},{8,24},{10,26},{12,28},{14,30},{16,0},... | collective-permute-start | bytes 294920 | tf_op jit(solution)/shard_map/ppermute | solution.py:23
  28.7 2.2 %copy-start.7 = (s32[96]{0:T(128)S(1)}, s32[96]{0:T(128)}, u32[]{:S(2)}) copy-start(s32[96]{0:T(128)} %param.17) | copy-start | bytes 1156
  28.8 4.3 %copy-start.4 = (f32[96]{0:T(128)S(1)}, f32[96]{0:T(128)}, u32[]{:S(2)}) copy-start(f32[96]{0:T(128)} %param.16) | copy-start | bytes 1156
  28.8 4.2 %copy-start.5 = (f32[96]{0:T(128)S(1)}, f32[96]{0:T(128)}, u32[]{:S(2)}) copy-start(f32[96]{0:T(128)} %param.15) | copy-start | bytes 1156
  28.8 4.2 %collective-permute-start.7 = (f32[96,128]{1,0:T(8,128)S(1)}, f32[96,128]{1,0:T(8,128)S(1)}, u32[]{:S(2)}, u32[]{:S(2)}) collective-permute-start(f32[96,128]{1,0:T(8,128)S(1)} %slice_select_fusion.2), channel_id=1, source_target_pairs={{0,8},{2,10},{4,12},{6,14},{8,0},{10,2},{12,4},{14,6},{16,24},{18,... | collective-permute-start | bytes 147464 | tf_op jit(solution)/shard_map/ppermute | solution.py:23
